TPU v7x, 32 devices: a whole 2x2x4 slice. The times are simulated.
32 devices in a mesh: fsdp: 2 (over x), ctx: 4 (over y, core), tp: 4 (over z).
Axes of the slice: x: 2, y: 2, z: 4, core: 2. Of those that a mesh axis runs over, the one named last changes fastest.
Arguments:
- tokens: bfloat16 [8, 1024, 2048], P('fsdp', 'ctx'), may hold values from -8 to 8
- positions: int32 [8, 1024], P('fsdp', 'ctx'), may hold values from 0 to 383, as said below
- block_ids: int32 [8, 1024], P('fsdp', 'ctx'), may hold values from 0 to 3, as said below
- gain_attend: bfloat16 [2048], P('fsdp'), may hold values from 0.099609375 to 1.8984375
- w_query: bfloat16 [2048, 2048], P('fsdp', 'tp'), may hold values from -0.125 to 0.125
- w_key: bfloat16 [2048, 2048], P('fsdp', 'tp'), may hold values from -0.125 to 0.125
- w_value: bfloat16 [2048, 2048], P('fsdp', 'tp'), may hold values from -0.125 to 0.125
- w_output: bfloat16 [2048, 2048], P('tp', 'fsdp'), may hold values from -1 to 1
- gain_feed: bfloat16 [2048], P('fsdp'), may hold values from 0.099609375 to 1.8984375
- w_gate: bfloat16 [2048, 8192], P('fsdp', 'tp'), may hold values from -0.125 to 0.125
- w_up: bfloat16 [2048, 8192], P('fsdp', 'tp'), may hold values from -0.125 to 0.125
- w_down: bfloat16 [8192, 2048], P('tp', 'fsdp'), may hold values from -0.0625 to 0.0625
- cotangent: bfloat16 [8, 1024, 2048], P('fsdp', 'ctx'), may hold values from -6 to 6
Outputs:
- layer_out: bfloat16 [8, 1024, 2048], P('fsdp', 'ctx')
- grad_input: bfloat16 [8, 1024, 2048], P('fsdp', 'ctx')
- grad_gain_attend: float32 [2048], P(('fsdp', 'ctx'))
- grad_w_query: float32 [2048, 2048], P(('fsdp', 'ctx'), 'tp')
- grad_w_key: float32 [2048, 2048], P(('fsdp', 'ctx'), 'tp')
- grad_w_value: float32 [2048, 2048], P(('fsdp', 'ctx'), 'tp')
- grad_w_output: float32 [2048, 2048], P('tp', ('fsdp', 'ctx'))
- grad_gain_feed: float32 [2048], P(('fsdp', 'ctx'))
- grad_w_gate: float32 [2048, 8192], P(('fsdp', 'ctx'), 'tp')
- grad_w_up: float32 [2048, 8192], P(('fsdp', 'ctx'), 'tp')
- grad_w_down: float32 [8192, 2048], P('tp', ('fsdp', 'ctx'))
- stream_rms: float32 [], replicated
- attend_rms: float32 [], replicated
- feed_rms: float32 [], replicated
Inputs may be any that keep to these rules, and one draw needn't show every extreme that they name: Along each sequence, positions count 0, 1, 2 and so on from the first token of each block, a run of equal block ids. `block_ids`: along each sequence block ids start at 0, never fall and rise by one at each new block.
All inputs are finite; a program needn't handle non-finite values.
Results may differ from a plain program's by a relative error of at most 0.015.
Values may be sent and summed in bfloat16 or wider, within the bound.
A program may use at most 256 MiB of HBM per device.

v0:
```python
import math
import jax
import jax.numpy as jnp
from jax import lax
from jax.sharding import PartitionSpec as P

HD = 128
norm_epsilon = 1e-05
rope_base = 10000.0


def plain_dot(left_side, right_side):
    return jnp.dot(left_side, right_side, preferred_element_type=jnp.float32)


def dot_last(left_side, right_side):
    return lax.dot_general(
        left_side, right_side, (((1,), (1,)), ((), ())), preferred_element_type=jnp.float32
    )


def dot_first(left_side, right_side):
    return lax.dot_general(
        left_side, right_side, (((0,), (0,)), ((), ())), preferred_element_type=jnp.float32
    )


def inverse_rms(values):
    return lax.rsqrt(jnp.mean(values * values, axis=-1, keepdims=True) + norm_epsilon)


def norm_back(grad_norm, values, scale_rows, gain):
    weighted = grad_norm * gain
    inner_mean = jnp.mean(weighted * values, axis=-1, keepdims=True)
    grad_values = (
        scale_rows * weighted - values * (scale_rows * scale_rows * scale_rows) * inner_mean
    )
    grad_gain = jnp.sum(grad_norm * (values * scale_rows), axis=0)
    return (grad_values, grad_gain)


def rope_tables(positions, head_size):
    half_size = head_size // 2
    inverse = jnp.exp(
        jnp.arange(half_size, dtype=jnp.float32) * (-2.0 * math.log(rope_base) / head_size)
    )
    turned = positions.astype(jnp.float32)[..., None, None] * inverse
    return (jnp.cos(turned), jnp.sin(turned))


def rotate(values, cosine, sine_table, direction):
    half_size = values.shape[-1] // 2
    first_half = values[..., :half_size]
    second_half = values[..., half_size:]
    return jnp.concatenate(
        [
            first_half * cosine - direction * (second_half * sine_table),
            direction * (first_half * sine_table) + second_half * cosine,
        ],
        axis=-1,
    )


def spread_rows(piece, ctx_size):
    part = piece.shape[0] // ctx_size
    mine = lax.dynamic_slice_in_dim(piece, lax.axis_index("ctx") * part, part, 0)
    return lax.all_gather(mine, ("fsdp", "ctx"), axis=0, tiled=True)


def spread_columns(piece, ctx_size):
    part = piece.shape[0] // ctx_size
    mine = lax.dynamic_slice_in_dim(piece, lax.axis_index("ctx") * part, part, 0)
    held = lax.all_gather(mine, ("fsdp", "ctx"), axis=0, tiled=True)
    fsdp_size = lax.axis_size("fsdp")
    held = held.reshape(fsdp_size, piece.shape[0], piece.shape[1])
    return jnp.swapaxes(held, 0, 1).reshape(piece.shape[0], fsdp_size * piece.shape[1])


def sum_rows(partial):
    return lax.psum_scatter(
        partial.astype(jnp.bfloat16), "tp", scatter_dimension=0, tiled=True
    ).astype(jnp.float32)


def every_row(rows):
    return lax.all_gather(rows, "tp", axis=0, tiled=True)


def local(
    tokens,
    positions,
    block_ids,
    gain_attend,
    w_query,
    w_key,
    w_value,
    w_output,
    gain_feed,
    w_gate,
    w_up,
    w_down,
    cotangent,
):
    seq_count, block_len, model_width = tokens.shape
    row_count = seq_count * block_len
    ctx_size = lax.axis_size("ctx")
    tp_size = lax.axis_size("tp")
    seq_len = block_len * ctx_size
    heads_here = w_query.shape[1] // HD
    width_here = heads_here * HD
    score_scale = 1.0 / math.sqrt(HD)
    score_shift = math.log(seq_len)
    shape_heads = (seq_count, block_len, heads_here, HD)
    low = jnp.bfloat16
    part_rows = row_count // tp_size
    row_at = lax.axis_index("tp") * part_rows
    token_rows = tokens.reshape(row_count, model_width)
    grad_rows = cotangent.reshape(row_count, model_width)
    token_part = lax.dynamic_slice_in_dim(token_rows, row_at, part_rows, 0).astype(jnp.float32)
    cotangent_part = lax.dynamic_slice_in_dim(grad_rows, row_at, part_rows, 0).astype(jnp.float32)
    qkv_full = spread_rows(jnp.concatenate([w_query, w_key, w_value], axis=1), ctx_size)
    gains = lax.all_gather(jnp.stack([gain_attend, gain_feed]), "fsdp", axis=1, tiled=True)
    gain_one = gains[0].astype(jnp.float32)
    gain_two = gains[1].astype(jnp.float32)
    output_full = spread_columns(w_output, ctx_size)
    gate_full = spread_rows(w_gate, ctx_size)
    up_full = spread_rows(w_up, ctx_size)
    down_full = spread_columns(w_down, ctx_size)
    stream = token_rows.astype(jnp.float32)
    scale_one = inverse_rms(stream)
    normed_one = (stream * scale_one * gain_one).astype(low)
    projected = plain_dot(normed_one, qkv_full)
    queries = projected[:, :width_here]
    key_proj = projected[:, width_here : 2 * width_here]
    values = projected[:, 2 * width_here :].astype(low)
    cosine, sine_table = rope_tables(positions, HD)
    query_rot = rotate(queries.reshape(shape_heads), cosine, sine_table, 1.0).astype(low)
    key_rot = rotate(key_proj.reshape(shape_heads), cosine, sine_table, 1.0).astype(low)
    key_value = lax.all_gather(
        jnp.concatenate(
            [
                key_rot.reshape(seq_count, block_len, width_here),
                values.reshape(seq_count, block_len, width_here),
            ],
            axis=2,
        ),
        "ctx",
        axis=1,
        tiled=True,
    )
    key_tags = lax.all_gather(block_ids, "ctx", axis=1, tiled=True)
    key_heads = key_value[:, :, :width_here].reshape(seq_count, seq_len, heads_here, HD)
    value_heads = key_value[:, :, width_here:].reshape(seq_count, seq_len, heads_here, HD)
    logits = (
        jnp.einsum("sqhd,skhd->shqk", query_rot, key_heads, preferred_element_type=jnp.float32)
        * score_scale
        - score_shift
    )
    allowed = key_tags[:, None, None, :] <= block_ids[:, None, :, None]
    squashed = jax.nn.sigmoid(logits)
    weights = jnp.where(allowed, squashed, 0.0).astype(low)
    attended = jnp.einsum(
        "shqk,skhd->sqhd", weights, value_heads, preferred_element_type=jnp.float32
    )
    mixed_rows = attended.reshape(row_count, width_here).astype(low)
    attend_part = sum_rows(plain_dot(mixed_rows, output_full))
    middle = token_part + attend_part
    scale_two = inverse_rms(middle)
    normed_two = every_row((middle * scale_two * gain_two).astype(low))
    gate_vals = plain_dot(normed_two, gate_full)
    up_vals = plain_dot(normed_two, up_full)
    gate_sig = jax.nn.sigmoid(gate_vals)
    gate_act = gate_vals * gate_sig
    hidden = (gate_act * up_vals).astype(low)
    grad_hidden = dot_last(grad_rows, down_full)
    slope = gate_sig * (1.0 + gate_vals * (1.0 - gate_sig))
    grad_gate = (grad_hidden * up_vals * slope).astype(low)
    grad_up = (grad_hidden * gate_act).astype(low)
    grad_normed_two = sum_rows(dot_last(grad_gate, gate_full) + dot_last(grad_up, up_full))
    feed_part = sum_rows(plain_dot(hidden, down_full))
    result = middle + feed_part
    layer_out = every_row(result.astype(low)).reshape(tokens.shape)
    grad_middle_norm, grad_gain_two = norm_back(grad_normed_two, middle, scale_two, gain_two)
    grad_middle = cotangent_part + grad_middle_norm
    grad_attend = every_row(grad_middle.astype(low))

    def scatter(value, dimension):
        return lax.psum_scatter(
            value.astype(low), ("fsdp", "ctx"), scatter_dimension=dimension, tiled=True
        ).astype(jnp.float32)

    grad_down = scatter(dot_first(hidden, grad_rows), 1)
    grad_gate_w = scatter(dot_first(normed_two, grad_gate), 0)
    grad_up_w = scatter(dot_first(normed_two, grad_up), 0)
    grad_mixed = dot_last(grad_attend, output_full).astype(low)
    grad_output_w = scatter(dot_first(mixed_rows, grad_attend), 1)
    grad_mixed_heads = grad_mixed.reshape(shape_heads)
    grad_weights = jnp.einsum(
        "sqhd,skhd->shqk", grad_mixed_heads, value_heads, preferred_element_type=jnp.float32
    )
    grad_logits = jnp.where(allowed, grad_weights * squashed * (1.0 - squashed), 0.0).astype(low)
    grad_query = score_scale * jnp.einsum(
        "shqk,skhd->sqhd", grad_logits, key_heads, preferred_element_type=jnp.float32
    )
    key_part = score_scale * jnp.einsum(
        "shqk,sqhd->skhd", grad_logits, query_rot, preferred_element_type=jnp.float32
    )
    value_part = jnp.einsum(
        "shqk,sqhd->skhd", weights, grad_mixed_heads, preferred_element_type=jnp.float32
    )
    pair = jnp.concatenate(
        [
            key_part.reshape(seq_count, seq_len, width_here).astype(low),
            value_part.reshape(seq_count, seq_len, width_here).astype(low),
        ],
        axis=2,
    )
    mine = lax.psum_scatter(pair, "ctx", scatter_dimension=1, tiled=True).astype(jnp.float32)
    grad_query_rows = rotate(grad_query, cosine, sine_table, -1.0).reshape(row_count, width_here)
    grad_key_rows = rotate(
        mine[:, :, :width_here].reshape(shape_heads), cosine, sine_table, -1.0
    ).reshape(row_count, width_here)
    grad_qkv = jnp.concatenate(
        [
            grad_query_rows.astype(low),
            grad_key_rows.astype(low),
            mine[:, :, width_here:].reshape(row_count, width_here).astype(low),
        ],
        axis=1,
    )
    grad_normed_one = sum_rows(dot_last(grad_qkv, qkv_full))
    grad_qkv_w = scatter(dot_first(normed_one, grad_qkv), 0)
    scale_one_part = lax.dynamic_slice_in_dim(scale_one, row_at, part_rows, 0)
    grad_input_norm, grad_gain_one = norm_back(
        grad_normed_one, token_part, scale_one_part, gain_one
    )
    grad_input = every_row((grad_middle + grad_input_norm).astype(low)).reshape(tokens.shape)
    sums = jnp.stack(
        [
            jnp.sum(result * result),
            jnp.sum(attend_part * attend_part),
            jnp.sum(feed_part * feed_part),
        ]
    )
    small = lax.psum(jnp.concatenate([grad_gain_one, grad_gain_two, sums]), ("fsdp", "ctx", "tp"))
    shards = lax.axis_size("fsdp") * ctx_size
    entries = float(row_count * model_width * shards)
    roots = jnp.sqrt(small[2 * model_width :] / entries)
    gain_part = model_width // shards
    gain_at = (lax.axis_index("fsdp") * ctx_size + lax.axis_index("ctx")) * gain_part
    grad_gain_attend = lax.dynamic_slice_in_dim(small, gain_at, gain_part, 0)
    grad_gain_feed = lax.dynamic_slice_in_dim(small, model_width + gain_at, gain_part, 0)
    return (
        layer_out,
        grad_input,
        grad_gain_attend,
        grad_qkv_w[:, :width_here],
        grad_qkv_w[:, width_here : 2 * width_here],
        grad_qkv_w[:, 2 * width_here :],
        grad_output_w,
        grad_gain_feed,
        grad_gate_w,
        grad_up_w,
        grad_down,
        roots[0],
        roots[1],
        roots[2],
    )


def solution(mesh):
    placed = (
        P("fsdp", "ctx", None),
        P("fsdp", "ctx"),
        P("fsdp", "ctx"),
        P("fsdp"),
        P("fsdp", "tp"),
        P("fsdp", "tp"),
        P("fsdp", "tp"),
        P("tp", "fsdp"),
        P("fsdp"),
        P("fsdp", "tp"),
        P("fsdp", "tp"),
        P("tp", "fsdp"),
        P("fsdp", "ctx", None),
    )
    return jax.shard_map(
        local,
        mesh=mesh,
        in_specs=placed,
        out_specs=(
            P("fsdp", "ctx", None),
            P("fsdp", "ctx", None),
            P(("fsdp", "ctx")),
            P(("fsdp", "ctx"), "tp"),
            P(("fsdp", "ctx"), "tp"),
            P(("fsdp", "ctx"), "tp"),
            P("tp", ("fsdp", "ctx")),
            P(("fsdp", "ctx")),
            P(("fsdp", "ctx"), "tp"),
            P(("fsdp", "ctx"), "tp"),
            P("tp", ("fsdp", "ctx")),
            P(),
            P(),
            P(),
        ),
        check_vma=False,
    )
```

profile of v0, /device:TPU:0, one launch (start us, length us, event | category | flops | bytes accessed | tf_op | source)
XLA Modules:
  0.0 1552.7 jit_solution(17306718815725621846)
XLA Ops:
  10.4 5.3 all_gather.36
  15.7 3.1 multiply_reduce_fusion
  21.3 37.3 %all-gather.11.cloned.1.call-done = bf16[2048,1536]{1,0:T(8,128)(2,1)} async-done(((bf16[256,1536]{1,0:T(8,128)(2,1)}), bf16[2048,1536]{1,0:T(8,128)(2,1)}) %all-gather.11.cloned.1.call-update) | async-done | bytes 6291472 | tf_op jit(solution)/shard_map/all_gather | solution.py:67
  58.7 10.1 fusion.23
  76.5 2.9 reshape.171
  79.4 4.6 fusion.43
  84.1 2.7 subtract_convert_fusion.2
  89.5 5.4 all_gather.39
  95.7 4.0 copy.66
  99.7 50.8 %all-gather.13.cloned.1.call-done = bf16[4,1024,1024]{1,2,0:T(8,128)(2,1)} async-done(((bf16[4,256,1024]{1,2,0:T(8,128)(2,1)}), bf16[4,1024,1024]{1,2,0:T(8,128)(2,1)}) %all-gather.13.cloned.1.call-update) | async-done | bytes 8388624 | tf_op jit(solution)/shard_map/all_gather | solution.py:139
  150.5 5.3 fusion.40
  155.8 8.5 add_divide_fusion
  164.3 10.0 fusion.21
  175.7 6.3 convolution_convert_fusion.6
  186.8 72.2 %reduce-scatter.11.cloned.1.call-done = bf16[256,2048]{1,0:T(8,128)(2,1)} async-done(((bf16[1024,2048]{1,0:T(8,128)(2,1)}), bf16[256,2048]{1,0:T(8,128)(2,1)}) %reduce-scatter.11.cloned.1.call-update) | async-done | bytes 1048592 | tf_op jit(solution)/shard_map/reduce_scatter | solution.py:80
  261.0 2.9 multiply_convert_fusion.3
  266.7 48.8 %all-gather.23.cloned.1.call-done = bf16[4096,1024]{1,0:T(8,128)(2,1)} async-done(((bf16[512,1024]{1,0:T(8,128)(2,1)}), bf16[4096,1024]{1,0:T(8,128)(2,1)}) %all-gather.23.cloned.1.call-update) | async-done | bytes 8388624 | tf_op jit(solution)/shard_map/all_gather | solution.py:73
  315.5 11.9 copy.67
  327.4 44.1 %all-gather.21.cloned.1.call-done = bf16[2048,2048]{1,0:T(8,128)(2,1)} async-done(((bf16[256,2048]{1,0:T(8,128)(2,1)}), bf16[2048,2048]{1,0:T(8,128)(2,1)}) %all-gather.21.cloned.1.call-update) | async-done | bytes 8388624 | tf_op jit(solution)/shard_map/all_gather | solution.py:67
  371.6 82.9 %all-gather.17.cloned.1.call-done = bf16[1024,2048]{1,0:T(8,128)(2,1)} async-done(((bf16[256,2048]{1,0:T(8,128)(2,1)}), bf16[1024,2048]{1,0:T(8,128)(2,1)}) %all-gather.17.cloned.1.call-update) | async-done | bytes 4194320 | tf_op jit(solution)/shard_map/all_gather | solution.py:86
  454.5 14.6 fusion.50
  469.0 40.7 %all-gather.19.cloned.1.call-done = bf16[2048,2048]{1,0:T(8,128)(2,1)} async-done(((bf16[256,2048]{1,0:T(8,128)(2,1)}), bf16[2048,2048]{1,0:T(8,128)(2,1)}) %all-gather.19.cloned.1.call-update) | async-done | bytes 8388624 | tf_op jit(solution)/shard_map/all_gather | solution.py:67
  509.7 14.7 fusion.49
  524.4 19.1 %fusion.2 = (bf16[1024,2048]{1,0:T(8,128)(2,1)}, bf16[1024,2048]{1,0:T(8,128)(2,1)}, bf16[1024,2048]{1,0:T(8,128)(2,1)}) fusion(f32[1024,2048]{1,0:T(8,128)} %fusion.49, f32[1024,2048]{1,0:T(8,128)} %fusion.50, bf16[1024,2048]{1,0:T(8,128)(2,1)S(1)} %bitcast.143, bf16[2048,2048]{0,1:T(8,128)(2,1)} %bitcast.121), kind=kOutput, calls=%fused_computation.8 | convolution fusion | flops 8621391872 | bytes 41943040 | tf_op jit(solution)/shard_map/dot_general | solution.py:17
  543.5 12.9 fusion.51
  556.4 12.9 add_convert_fusion
  569.3 14.0 convolution_convert_fusion.5
  583.6 62.6 %reduce-scatter.15.cloned.1.call-done = bf16[256,2048]{1,0:T(8,128)(2,1)} async-done(((bf16[1024,2048]{1,0:T(8,128)(2,1)}), bf16[256,2048]{1,0:T(8,128)(2,1)}) %reduce-scatter.15.cloned.1.call-update) | async-done | bytes 1048592 | tf_op jit(solution)/shard_map/reduce_scatter | solution.py:80
  646.2 79.4 %reduce-scatter.13.cloned.1.call-done = bf16[256,2048]{1,0:T(8,128)(2,1)} async-done(((bf16[1024,2048]{1,0:T(8,128)(2,1)}), bf16[256,2048]{1,0:T(8,128)(2,1)}) %reduce-scatter.13.cloned.1.call-update) | async-done | bytes 1048592 | tf_op jit(solution)/shard_map/reduce_scatter | solution.py:80
  725.7 5.1 fusion.16
  730.8 3.4 fusion.39
  734.2 81.4 %all-gather.27.cloned.1.call-done = bf16[1024,2048]{1,0:T(8,128)(2,1)} async-done(((bf16[256,2048]{1,0:T(8,128)(2,1)}), bf16[1024,2048]{1,0:T(8,128)(2,1)}) %all-gather.27.cloned.1.call-update) | async-done | bytes 4194320 | tf_op jit(solution)/shard_map/all_gather | solution.py:86
  815.6 6.2 convolution_convert_fusion.9
  826.2 9.5 select_convert_fusion
  835.7 12.9 convolution_convert_fusion.8
  848.6 5.9 multiply_convert_fusion
  854.4 7.7 pad_maximum_fusion
  862.7 7.7 multiply_bitcast_fusion
  870.4 61.7 %reduce-scatter.17.cloned.1.call-done = bf16[4,256,1024]{1,2,0:T(8,128)(2,1)} async-done(((bf16[4,1024,1024]{1,2,0:T(8,128)(2,1)}), bf16[4,256,1024]{1,2,0:T(8,128)(2,1)}) %reduce-scatter.17.cloned.1.call-update) | async-done | bytes 2097168 | tf_op jit(solution)/shard_map/reduce_scatter | solution.py:218
  932.1 3.0 fusion.42
  937.4 2.8 fusion.45
  940.2 3.2 copy.88
  943.3 3.2 copy.89
  946.5 3.5 subtract_convert_fusion.1
  954.2 8.2 convolution_convert_fusion.4
  962.7 14.1 convolution_convert_fusion
  976.9 14.2 convolution_convert_fusion.1
  991.4 14.0 convolution_convert_fusion.2
  1006.6 5.9 convolution_convert_fusion.7
  1012.6 11.2 convolution_convert_fusion.3
  1024.5 14.9 reduce-scatter.19.cloned.1.call-done
  1042.0 4.3 fusion.10
  1046.4 68.2 %reduce-scatter.29.cloned.1.call-done = bf16[2048,256]{1,0:T(8,128)(2,1)} async-done(((bf16[2048,2048]{1,0:T(8,128)(2,1)}), bf16[2048,256]{1,0:T(8,128)(2,1)}) %reduce-scatter.29.cloned.1.call-update) | async-done | bytes 1048592 | tf_op jit(solution)/shard_map/reduce_scatter | solution.py:188
  1114.6 2.7 convert_element_type.201
  1117.3 72.1 %reduce-scatter.27.cloned.1.call-done = bf16[256,2048]{1,0:T(8,128)(2,1)} async-done(((bf16[2048,2048]{1,0:T(8,128)(2,1)}), bf16[256,2048]{1,0:T(8,128)(2,1)}) %reduce-scatter.27.cloned.1.call-update) | async-done | bytes 1048592 | tf_op jit(solution)/shard_map/reduce_scatter | solution.py:188
  1189.4 2.8 convert_element_type.199
  1192.2 72.0 %reduce-scatter.25.cloned.1.call-done = bf16[256,2048]{1,0:T(8,128)(2,1)} async-done(((bf16[2048,2048]{1,0:T(8,128)(2,1)}), bf16[256,2048]{1,0:T(8,128)(2,1)}) %reduce-scatter.25.cloned.1.call-update) | async-done | bytes 1048592 | tf_op jit(solution)/shard_map/reduce_scatter | solution.py:188
  1264.3 2.8 convert_element_type.197
  1267.1 79.4 %all-gather.25.cloned.1.call-done = bf16[1024,2048]{1,0:T(8,128)(2,1)} async-done(((bf16[256,2048]{1,0:T(8,128)(2,1)}), bf16[1024,2048]{1,0:T(8,128)(2,1)}) %all-gather.25.cloned.1.call-update) | async-done | bytes 4194320 | tf_op jit(solution)/shard_map/all_gather | solution.py:86
  1346.5 43.4 %reduce-scatter.23.cloned.1.call-done = bf16[512,256]{1,0:T(8,128)(2,1)} async-done(((bf16[512,2048]{1,0:T(8,128)(2,1)}), bf16[512,256]{1,0:T(8,128)(2,1)}) %reduce-scatter.23.cloned.1.call-update) | async-done | bytes 262160 | tf_op jit(solution)/shard_map/reduce_scatter | solution.py:188
  1393.6 40.0 %psum.7 = f32[4099]{0:T(1024)S(1)} all-reduce(f32[4099]{0:T(1024)S(1)} %concatenate.39), channel_id=1, replica_groups=mesh['fsdp'=2,'ctx'=4,'tp'=4] {'fsdp','ctx','tp'}, use_global_device_ids=true, to_apply=%region_14.15 | all-reduce | flops 4099 | bytes 32792 | tf_op jit(solution)/shard_map/psum | solution.py:245
  1434.8 20.8 %reduce-scatter.21.cloned.1.call-done = bf16[256,1536]{1,0:T(8,128)(2,1)} async-done(((bf16[2048,1536]{1,0:T(8,128)(2,1)}), bf16[256,1536]{1,0:T(8,128)(2,1)}) %reduce-scatter.21.cloned.1.call-update) | async-done | bytes 786448 | tf_op jit(solution)/shard_map/reduce_scatter | solution.py:188
  1458.0 80.4 %all-gather.29.cloned.1.call-done = bf16[1024,2048]{1,0:T(8,128)(2,1)} async-done(((bf16[256,2048]{1,0:T(8,128)(2,1)}), bf16[1024,2048]{1,0:T(8,128)(2,1)}) %all-gather.29.cloned.1.call-update) | async-done | bytes 4194320 | tf_op jit(solution)/shard_map/all_gather | solution.py:86
  1538.5 4.9 copy.117
  (148 shorter events, 53.8 us)
Async XLA Ops:
  7.2 2.3 copy-start
  7.2 3.1 copy-start.22
  7.2 3.1 copy-start.25
  7.2 3.1 copy-start.26
  7.2 51.4 %all-gather.11.cloned.1.call-start = ((), (), s32[]{:S(2)}) async-start(), calls=%async_computation.10 | async-start | bytes 7077888 | tf_op jit(solution)/shard_map/all_gather | solution.py:67
  9.4 86.2 %all-gather.15.cloned.1.call-start = ((), (), s32[]{:S(2)}) async-start(), calls=%async_computation.12 | async-start | bytes 2359296 | tf_op jit(solution)/shard_map/all_gather | solution.py:73
  10.2 140.2 %all-gather.13.cloned.1.call-start = ((), (), s32[]{:S(2)}) async-start(), calls=%async_computation.11 | async-start | bytes 10485760 | tf_op jit(solution)/shard_map/all_gather | solution.py:139
  19.4 49.4 %copy-start.23 = (f32[1,2,4,128]{3,1,2,0:T(2,128)}, f32[1,2,4,128]{3,1,2,0:T(2,128)S(1)}, u32[]{:S(2)}) copy-start(f32[1,2,4,128]{3,1,2,0:T(2,128)S(1)} %copy.90) | copy-start | bytes 12292
  19.4 49.4 %copy-start.18 = (f32[1,2048]{1,0:T(1,128)}, f32[1,2048]{1,0:T(1,128)S(1)}, u32[]{:S(2)}) copy-start(f32[1,2048]{1,0:T(1,128)S(1)} %get-tuple-element.57) | copy-start | bytes 24580
  21.3 62.8 %copy-start.7 = (f32[4,256,64]{2,1,0:T(8,128)}, f32[4,256,64]{2,1,0:T(8,128)S(1)}, u32[]{:S(2)}) copy-start(f32[4,256,64]{2,1,0:T(8,128)S(1)} %get-tuple-element.58) | copy-start | bytes 786436
  21.3 62.8 %copy-start.8 = (f32[4,256,64]{2,1,0:T(8,128)}, f32[4,256,64]{2,1,0:T(8,128)S(1)}, u32[]{:S(2)}) copy-start(f32[4,256,64]{2,1,0:T(8,128)S(1)} %get-tuple-element.59) | copy-start | bytes 786436
  86.8 1.2 copy-start.12
  87.4 2.2 copy-start.20
  89.5 169.5 %reduce-scatter.11.cloned.1.call-start = ((), (), s32[]{:S(2)}) async-start(), calls=%async_computation.13 | async-start | bytes 5242880 | tf_op jit(solution)/shard_map/reduce_scatter | solution.py:80
  99.6 56.1 %copy-start.9 = (bf16[4,256,4,64]{3,1,2,0:T(8,128)(2,1)S(1)}, bf16[4,256,4,64]{3,1,2,0:T(8,128)(2,1)}, u32[]{:S(2)}) copy-start(bf16[4,256,4,64]{3,1,2,0:T(8,128)(2,1)} %get-tuple-element.32) | copy-start | bytes 1572868
  150.5 5.3 copy-start.10
  155.8 8.5 copy-start.4
  182.0 133.5 %all-gather.23.cloned.1.call-start = ((), (), s32[]{:S(2)}) async-start(), calls=%async_computation.17 | async-start | bytes 9437184 | tf_op jit(solution)/shard_map/all_gather | solution.py:73
  184.4 187.2 %all-gather.21.cloned.1.call-start = ((), (), s32[]{:S(2)}) async-start(), calls=%async_computation.16 | async-start | bytes 9437184 | tf_op jit(solution)/shard_map/all_gather | solution.py:67
  186.8 267.7 %all-gather.17.cloned.1.call-start = ((), (), s32[]{:S(2)}) async-start(), calls=%async_computation.14 | async-start | bytes 5242880 | tf_op jit(solution)/shard_map/all_gather | solution.py:86
  263.9 245.8 %all-gather.19.cloned.1.call-start = ((), (), s32[]{:S(2)}) async-start(), calls=%async_computation.15 | async-start | bytes 9437184 | tf_op jit(solution)/shard_map/all_gather | solution.py:67
  266.3 379.9 %reduce-scatter.15.cloned.1.call-start = ((), (), s32[]{:S(2)}) async-start(), calls=%async_computation.20 | async-start | bytes 5242880 | tf_op jit(solution)/shard_map/reduce_scatter | solution.py:80
  509.7 14.7 copy-start.17
  543.5 12.9 copy-start.27
  569.3 156.4 %reduce-scatter.13.cloned.1.call-start = ((), (), s32[]{:S(2)}) async-start(), calls=%async_computation.18 | async-start | bytes 5242880 | tf_op jit(solution)/shard_map/reduce_scatter | solution.py:80
  583.3 142.4 %copy-start.3 = (bf16[256,2048]{1,0:T(8,128)(2,1)S(1)}, bf16[256,2048]{1,0:T(8,128)(2,1)}, u32[]{:S(2)}) copy-start(bf16[256,2048]{1,0:T(8,128)(2,1)} %reduce-scatter.11.cloned.1.call-done) | copy-start | bytes 3145732
  583.3 232.3 %all-gather.27.cloned.1.call-start = ((), (), s32[]{:S(2)}) async-start(), calls=%async_computation.21 | async-start | bytes 5242880 | tf_op jit(solution)/shard_map/all_gather | solution.py:86
  725.7 5.1 copy-start.5
  734.2 197.9 %reduce-scatter.17.cloned.1.call-start = ((), (), s32[]{:S(2)}) async-start(), calls=%async_computation.22 | async-start | bytes 10485760 | tf_op jit(solution)/shard_map/reduce_scatter | solution.py:218
  835.6 12.9 copy-start.2
  862.2 177.2 %reduce-scatter.19.cloned.1.call-start = ((), (), s32[]{:S(2)}) async-start(), calls=%async_computation.23 | async-start | bytes 5242880 | tf_op jit(solution)/shard_map/reduce_scatter | solution.py:80
  946.5 7.8 slice-start
  950.0 4.2 slice-start.1
  951.6 1.6 copy-start.15
  951.6 2.6 copy-start.14
  953.2 1.0 copy-start.16
  962.5 152.1 %reduce-scatter.29.cloned.1.call-start = ((), (), s32[]{:S(2)}) async-start(), calls=%async_computation.29 | async-start | bytes 9437184 | tf_op jit(solution)/shard_map/reduce_scatter | solution.py:188
  976.8 212.6 %reduce-scatter.27.cloned.1.call-start = ((), (), s32[]{:S(2)}) async-start(), calls=%async_computation.28 | async-start | bytes 9437184 | tf_op jit(solution)/shard_map/reduce_scatter | solution.py:188
  991.1 273.2 %reduce-scatter.25.cloned.1.call-start = ((), (), s32[]{:S(2)}) async-start(), calls=%async_computation.27 | async-start | bytes 9437184 | tf_op jit(solution)/shard_map/reduce_scatter | solution.py:188
  1005.4 1.2 copy-start.13
  1005.4 341.0 %all-gather.25.cloned.1.call-start = ((), (), s32[]{:S(2)}) async-start(), calls=%async_computation.19 | async-start | bytes 5242880 | tf_op jit(solution)/shard_map/all_gather | solution.py:86
  1006.0 6.6 copy-start.19
  1006.0 6.6 copy-start.24
  1006.0 383.8 %reduce-scatter.23.cloned.1.call-start = ((), (), s32[]{:S(2)}) async-start(), calls=%async_computation.26 | async-start | bytes 2359296 | tf_op jit(solution)/shard_map/reduce_scatter | solution.py:188
  1012.5 443.1 %reduce-scatter.21.cloned.1.call-start = ((), (), s32[]{:S(2)}) async-start(), calls=%async_computation.25 | async-start | bytes 7077888 | tf_op jit(solution)/shard_map/reduce_scatter | solution.py:188
  1023.9 0.7 copy-start.21
  1023.9 18.2 %copy-start.6 = (bf16[256,2048]{1,0:T(8,128)(2,1)S(1)}, bf16[256,2048]{1,0:T(8,128)(2,1)}, u32[]{:S(2)}) copy-start(bf16[256,2048]{1,0:T(8,128)(2,1)} %reduce-scatter.15.cloned.1.call-done) | copy-start | bytes 3145732
  1023.9 514.6 %all-gather.29.cloned.1.call-start = ((), (), s32[]{:S(2)}) async-start(), calls=%async_computation.24 | async-start | bytes 5242880 | tf_op jit(solution)/shard_map/all_gather | solution.py:86
  1538.4 4.9 copy-start.11
  1538.5 7.0 copy-start.1
Sparse Core Ops, SparseCore 0:
  10.5 48.1 all-gather.10
  61.1 27.7 all-gather.14
  91.1 59.3 all-gather.12
  182.2 76.7 reduce-scatter.10
  260.7 54.7 all-gather.22
  317.3 54.2 all-gather.20
  373.7 80.7 all-gather.16
  456.9 52.7 all-gather.18
  569.4 76.7 reduce-scatter.14
  648.3 77.2 reduce-scatter.12
  734.3 81.2 all-gather.26
  862.3 69.7 reduce-scatter.16
  962.6 76.7 reduce-scatter.18
  1042.8 71.7 reduce-scatter.28
  1117.9 71.4 reduce-scatter.26
  1192.7 71.4 reduce-scatter.24
  1265.7 80.7 all-gather.24
  1350.2 39.6 reduce-scatter.22
  1393.2 62.4 reduce-scatter.20
  1457.7 80.7 all-gather.28
where the time goes:
time: 1560 us; the launch traced here: 1550 us
  waiting for transfers between devices  1110 us (71%)
  matrix products  233 us (15%)
  local copies, waits for them, and re-layouts  81.4 us (5%)
  other arithmetic  55.9 us (4%)
  blocking collectives  50.7 us (3%)
    all_gather x4, waiting for transfers between devices, every_row(): return lax.all_gather(rows, 'tp', axis=0, tiled=True)  324 us
    reduce_scatter x5, waiting for transfers between devices, scatter(): lax.psum_scatter(value.astype(low), ('fsdp', 'ctx'), scatter_dimension=di...  277 us
    reduce_scatter x4, waiting for transfers between devices, sum_rows(): lax.psum_scatter(partial.astype(jnp.bfloat16), 'tp', scatter_dimension=0,...  229 us
    all_gather x3, waiting for transfers between devices, spread_rows(): return lax.all_gather(mine, ('fsdp', 'ctx'), axis=0, tiled=True)  122 us
    reduce_scatter x1, waiting for transfers between devices, local(): lax.psum_scatter(pair, 'ctx', scatter_dimension=1, tiled=True)  61.7 us
    dot_general x5, matrix products, plain_dot(): return jnp.dot(left_side, right_side, preferred_element_type=jnp.float32)  59.6 us
    dot_general x5, matrix products, dot_first(): lax.dot_general(left_side, right_side, (((0,), (0,)), ((), ())), preferre...  59.5 us
    dot_general x5, matrix products, dot_last(): lax.dot_general(left_side, right_side, (((1,), (1,)), ((), ())), preferre...  59.2 us
  transfers between devices with their start and end apart: 20, of which 19 were waited for; matrix products, arithmetic and copies ran while one was open for 12% of the time, Pallas kernels for 0%

commit v1 on v0

--- a/solution.py
+++ b/solution.py
@@ -1,3 +1,4 @@
+import functools
 import math
 import jax
 import jax.numpy as jnp
@@ -7,6 +8,13 @@
 HD = 128
 norm_epsilon = 1e-05
 rope_base = 10000.0
+
+
+def derive_slots_up(payload, net_axis):
+    return jax.lax.all_gather(payload, net_axis).sum(axis=0)
+
+
+match_the_rates = functools.partial(derive_slots_up, net_axis=("fsdp", "ctx", "tp"))
 
 
 def plain_dot(left_side, right_side):
@@ -242,7 +250,7 @@
             jnp.sum(feed_part * feed_part),
         ]
     )
-    small = lax.psum(jnp.concatenate([grad_gain_one, grad_gain_two, sums]), ("fsdp", "ctx", "tp"))
+    small = match_the_rates(jnp.concatenate([grad_gain_one, grad_gain_two, sums]))
     shards = lax.axis_size("fsdp") * ctx_size
     entries = float(row_count * model_width * shards)
     roots = jnp.sqrt(small[2 * model_width :] / entries)

time: 1560 us -> 1680 us (1.077)
  waiting for transfers between devices: 1110 us -> 1270 us
  blocking collectives: 50.7 us -> 10.7 us
    unnamed x20 -> x22, waiting for transfers between devices: 0.84 us -> 132 us
    psum x1 -> x0, blocking collectives: 40 us -> none  [local(): lax.psum(jnp.concatenate([grad_gain_one, grad_gain_two, sums]), ('fsdp',...]
    reduce_scatter x5, waiting for transfers between devices: 277 us -> 303 us  [scatter(): lax.psum_scatter(value.astype(low), ('fsdp', 'ctx'), scatter_dimension=di...]
  transfers between devices with their start and end apart: 20 -> 21, of which waited for: 19 -> 20; matrix products, arithmetic and copies ran while one was open for 12% -> 12% of each run, Pallas kernels for 0% -> 0%
where the time goes in v1:
time: 1680 us; the launch traced here: 1670 us
  waiting for transfers between devices  1270 us (76%)
  matrix products  235 us (14%)
  local copies, waits for them, and re-layouts  81.1 us (5%)
  other arithmetic  55.6 us (3%)
    all_gather x4, waiting for transfers between devices, every_row(): return lax.all_gather(rows, 'tp', axis=0, tiled=True)  324 us
    reduce_scatter x5, waiting for transfers between devices, scatter(): lax.psum_scatter(value.astype(low), ('fsdp', 'ctx'), scatter_dimension=di...  303 us
    reduce_scatter x4, waiting for transfers between devices, sum_rows(): lax.psum_scatter(partial.astype(jnp.bfloat16), 'tp', scatter_dimension=0,...  229 us
    unnamed x22, waiting for transfers between devices  132 us
    all_gather x3, waiting for transfers between devices, spread_rows(): return lax.all_gather(mine, ('fsdp', 'ctx'), axis=0, tiled=True)  122 us
    reduce_scatter x1, waiting for transfers between devices, local(): lax.psum_scatter(pair, 'ctx', scatter_dimension=1, tiled=True)  61.7 us
    dot_general x5, matrix products, dot_last(): lax.dot_general(left_side, right_side, (((1,), (1,)), ((), ())), preferre...  61.5 us
    dot_general x5, matrix products, plain_dot(): return jnp.dot(left_side, right_side, preferred_element_type=jnp.float32)  59.8 us
  transfers between devices with their start and end apart: 21, of which 20 were waited for; matrix products, arithmetic and copies ran while one was open for 12% of the time, Pallas kernels for 0%

profile of v1, /device:TPU:0, one launch (start us, length us, event | category | flops | bytes accessed | tf_op | source)
XLA Modules:
  0.0 1673.9 jit_solution(3732665813783324318)
XLA Ops:
  10.4 5.3 all_gather.42
  15.7 3.1 multiply_reduce_fusion
  21.3 37.3 %all-gather.12.cloned.1.call-done = bf16[2048,1536]{1,0:T(8,128)(2,1)} async-done(((bf16[256,1536]{1,0:T(8,128)(2,1)}), bf16[2048,1536]{1,0:T(8,128)(2,1)}) %all-gather.12.cloned.1.call-update) | async-done | bytes 6291472 | tf_op jit(solution)/shard_map/all_gather | solution.py:75
  58.6 10.1 fusion.23
  74.3 2.9 reshape.174
  77.2 4.7 fusion.43
  81.9 2.7 subtract_convert_fusion.2
  87.9 5.4 all_gather.45
  94.0 4.0 copy.87
  98.0 52.5 %all-gather.14.cloned.1.call-done = bf16[4,1024,1024]{1,2,0:T(8,128)(2,1)} async-done(((bf16[4,256,1024]{1,2,0:T(8,128)(2,1)}), bf16[4,1024,1024]{1,2,0:T(8,128)(2,1)}) %all-gather.14.cloned.1.call-update) | async-done | bytes 8388624 | tf_op jit(solution)/shard_map/all_gather | solution.py:147
  150.5 5.3 fusion.40
  155.8 8.5 add_divide_fusion
  164.3 10.0 fusion.21
  175.7 6.3 convolution_convert_fusion.6
  186.8 72.1 %reduce-scatter.11.cloned.1.call-done = bf16[256,2048]{1,0:T(8,128)(2,1)} async-done(((bf16[1024,2048]{1,0:T(8,128)(2,1)}), bf16[256,2048]{1,0:T(8,128)(2,1)}) %reduce-scatter.11.cloned.1.call-update) | async-done | bytes 1048592 | tf_op jit(solution)/shard_map/reduce_scatter | solution.py:88
  260.9 2.9 multiply_convert_fusion.3
  266.7 48.8 %all-gather.24.cloned.1.call-done = bf16[4096,1024]{1,0:T(8,128)(2,1)} async-done(((bf16[512,1024]{1,0:T(8,128)(2,1)}), bf16[4096,1024]{1,0:T(8,128)(2,1)}) %all-gather.24.cloned.1.call-update) | async-done | bytes 8388624 | tf_op jit(solution)/shard_map/all_gather | solution.py:81
  315.5 11.9 copy.88
  327.4 44.1 %all-gather.22.cloned.1.call-done = bf16[2048,2048]{1,0:T(8,128)(2,1)} async-done(((bf16[256,2048]{1,0:T(8,128)(2,1)}), bf16[2048,2048]{1,0:T(8,128)(2,1)}) %all-gather.22.cloned.1.call-update) | async-done | bytes 8388624 | tf_op jit(solution)/shard_map/all_gather | solution.py:75
  371.5 82.9 %all-gather.18.cloned.1.call-done = bf16[1024,2048]{1,0:T(8,128)(2,1)} async-done(((bf16[256,2048]{1,0:T(8,128)(2,1)}), bf16[1024,2048]{1,0:T(8,128)(2,1)}) %all-gather.18.cloned.1.call-update) | async-done | bytes 4194320 | tf_op jit(solution)/shard_map/all_gather | solution.py:94
  454.4 14.6 fusion.50
  469.0 40.7 %all-gather.20.cloned.1.call-done = bf16[2048,2048]{1,0:T(8,128)(2,1)} async-done(((bf16[256,2048]{1,0:T(8,128)(2,1)}), bf16[2048,2048]{1,0:T(8,128)(2,1)}) %all-gather.20.cloned.1.call-update) | async-done | bytes 8388624 | tf_op jit(solution)/shard_map/all_gather | solution.py:75
  509.7 14.7 fusion.49
  524.4 19.1 %fusion.2 = (bf16[1024,2048]{1,0:T(8,128)(2,1)}, bf16[1024,2048]{1,0:T(8,128)(2,1)}, bf16[1024,2048]{1,0:T(8,128)(2,1)}) fusion(f32[1024,2048]{1,0:T(8,128)} %fusion.49, f32[1024,2048]{1,0:T(8,128)} %fusion.50, bf16[1024,2048]{1,0:T(8,128)(2,1)S(1)} %bitcast.143, bf16[2048,2048]{0,1:T(8,128)(2,1)} %bitcast.121), kind=kOutput, calls=%fused_computation.8 | convolution fusion | flops 8621391872 | bytes 41943040 | tf_op jit(solution)/shard_map/dot_general | solution.py:25
  543.4 14.1 convolution_convert_fusion.5
  557.6 12.7 fusion.51
  570.4 12.9 add_convert_fusion
  583.5 51.0 %reduce-scatter.13.cloned.1.call-done = bf16[256,2048]{1,0:T(8,128)(2,1)} async-done(((bf16[1024,2048]{1,0:T(8,128)(2,1)}), bf16[256,2048]{1,0:T(8,128)(2,1)}) %reduce-scatter.13.cloned.1.call-update) | async-done | bytes 1048592 | tf_op jit(solution)/shard_map/reduce_scatter | solution.py:88
  634.5 79.4 %reduce-scatter.15.cloned.1.call-done = bf16[256,2048]{1,0:T(8,128)(2,1)} async-done(((bf16[1024,2048]{1,0:T(8,128)(2,1)}), bf16[256,2048]{1,0:T(8,128)(2,1)}) %reduce-scatter.15.cloned.1.call-update) | async-done | bytes 1048592 | tf_op jit(solution)/shard_map/reduce_scatter | solution.py:88
  714.0 5.1 fusion.16
  719.1 3.4 fusion.39
  722.5 81.4 %all-gather.28.cloned.1.call-done = bf16[1024,2048]{1,0:T(8,128)(2,1)} async-done(((bf16[256,2048]{1,0:T(8,128)(2,1)}), bf16[1024,2048]{1,0:T(8,128)(2,1)}) %all-gather.28.cloned.1.call-update) | async-done | bytes 4194320 | tf_op jit(solution)/shard_map/all_gather | solution.py:94
  803.9 6.2 convolution_convert_fusion.9
  814.5 9.5 select_convert_fusion
  824.0 12.9 convolution_convert_fusion.8
  836.9 5.9 multiply_convert_fusion
  842.8 7.7 pad_maximum_fusion
  851.0 7.7 multiply_bitcast_fusion
  858.7 61.7 %reduce-scatter.17.cloned.1.call-done = bf16[4,256,1024]{1,2,0:T(8,128)(2,1)} async-done(((bf16[4,1024,1024]{1,2,0:T(8,128)(2,1)}), bf16[4,256,1024]{1,2,0:T(8,128)(2,1)}) %reduce-scatter.17.cloned.1.call-update) | async-done | bytes 2097168 | tf_op jit(solution)/shard_map/reduce_scatter | solution.py:226
  920.4 2.6 fusion.42
  924.6 3.2 copy.109
  927.8 3.2 copy.110
  930.9 3.4 subtract_convert_fusion.1
  939.8 10.7 convolution_convert_fusion.4
  950.8 14.1 convolution_convert_fusion.2
  965.0 14.1 convolution_convert_fusion.1
  979.4 14.1 convolution_convert_fusion
  994.7 5.9 convolution_convert_fusion.7
  1000.8 26.7 %reduce-scatter.19.cloned.1.call-done = bf16[256,2048]{1,0:T(8,128)(2,1)} async-done(((bf16[1024,2048]{1,0:T(8,128)(2,1)}), bf16[256,2048]{1,0:T(8,128)(2,1)}) %reduce-scatter.19.cloned.1.call-update) | async-done | bytes 1048592 | tf_op jit(solution)/shard_map/reduce_scatter | solution.py:88
  1027.5 2.6 fusion.17
  1033.5 11.3 convolution_convert_fusion.3
  1046.7 4.1 fusion.10
  1050.8 52.0 %reduce-scatter.25.cloned.1.call-done = bf16[256,2048]{1,0:T(8,128)(2,1)} async-done(((bf16[2048,2048]{1,0:T(8,128)(2,1)}), bf16[256,2048]{1,0:T(8,128)(2,1)}) %reduce-scatter.25.cloned.1.call-update) | async-done | bytes 1048592 | tf_op jit(solution)/shard_map/reduce_scatter | solution.py:196
  1102.9 2.8 convert_element_type.197
  1105.7 72.0 %reduce-scatter.27.cloned.1.call-done = bf16[256,2048]{1,0:T(8,128)(2,1)} async-done(((bf16[2048,2048]{1,0:T(8,128)(2,1)}), bf16[256,2048]{1,0:T(8,128)(2,1)}) %reduce-scatter.27.cloned.1.call-update) | async-done | bytes 1048592 | tf_op jit(solution)/shard_map/reduce_scatter | solution.py:196
  1177.7 2.8 convert_element_type.199
  1180.5 71.8 %reduce-scatter.29.cloned.1.call-done = bf16[2048,256]{1,0:T(8,128)(2,1)} async-done(((bf16[2048,2048]{1,0:T(8,128)(2,1)}), bf16[2048,256]{1,0:T(8,128)(2,1)}) %reduce-scatter.29.cloned.1.call-update) | async-done | bytes 1048592 | tf_op jit(solution)/shard_map/reduce_scatter | solution.py:196
  1252.3 2.7 convert_element_type.201
  1255.0 79.5 %all-gather.26.cloned.1.call-done = bf16[1024,2048]{1,0:T(8,128)(2,1)} async-done(((bf16[256,2048]{1,0:T(8,128)(2,1)}), bf16[1024,2048]{1,0:T(8,128)(2,1)}) %all-gather.26.cloned.1.call-update) | async-done | bytes 4194320 | tf_op jit(solution)/shard_map/all_gather | solution.py:94
  1334.5 43.4 %reduce-scatter.23.cloned.1.call-done = bf16[512,256]{1,0:T(8,128)(2,1)} async-done(((bf16[512,2048]{1,0:T(8,128)(2,1)}), bf16[512,256]{1,0:T(8,128)(2,1)}) %reduce-scatter.23.cloned.1.call-update) | async-done | bytes 262160 | tf_op jit(solution)/shard_map/reduce_scatter | solution.py:196
  1379.6 131.1 %all-reduce.3.cloned.1.call-done = f32[131168]{0:T(1024)} async-done(((f32[131168]{0:T(1024)}), f32[131168]{0:T(1024)}) %all-reduce.3.cloned.1.call-update) | async-done | bytes 524688
  1513.5 63.3 %reduce-scatter.21.cloned.1.call-done = bf16[256,1536]{1,0:T(8,128)(2,1)} async-done(((bf16[2048,1536]{1,0:T(8,128)(2,1)}), bf16[256,1536]{1,0:T(8,128)(2,1)}) %reduce-scatter.21.cloned.1.call-update) | async-done | bytes 786448 | tf_op jit(solution)/shard_map/reduce_scatter | solution.py:196
  1579.1 80.6 %all-gather.30.cloned.1.call-done = bf16[1024,2048]{1,0:T(8,128)(2,1)} async-done(((bf16[256,2048]{1,0:T(8,128)(2,1)}), bf16[1024,2048]{1,0:T(8,128)(2,1)}) %all-gather.30.cloned.1.call-update) | async-done | bytes 4194320 | tf_op jit(solution)/shard_map/all_gather | solution.py:94
  1659.7 4.9 copy.140
  (149 shorter events, 54.1 us)
Async XLA Ops:
  7.2 2.3 copy-start
  7.2 3.1 copy-start.25
  7.2 3.1 copy-start.26
  7.2 51.4 %all-gather.12.cloned.1.call-start = ((), (), s32[]{:S(2)}) async-start(), calls=%async_computation.10 | async-start | bytes 7077888 | tf_op jit(solution)/shard_map/all_gather | solution.py:75
  7.3 12.1 copy-start.22
  9.4 84.5 %all-gather.16.cloned.1.call-start = ((), (), s32[]{:S(2)}) async-start(), calls=%async_computation.12 | async-start | bytes 2359296 | tf_op jit(solution)/shard_map/all_gather | solution.py:81
  10.2 140.2 %all-gather.14.cloned.1.call-start = ((), (), s32[]{:S(2)}) async-start(), calls=%async_computation.11 | async-start | bytes 10485760 | tf_op jit(solution)/shard_map/all_gather | solution.py:147
  15.7 53.1 %copy-start.18 = (f32[1,2048]{1,0:T(1,128)}, f32[1,2048]{1,0:T(1,128)S(1)}, u32[]{:S(2)}) copy-start(f32[1,2048]{1,0:T(1,128)S(1)} %get-tuple-element.57) | copy-start | bytes 24580
  19.4 49.4 %copy-start.23 = (f32[1,2,4,128]{3,1,2,0:T(2,128)}, f32[1,2,4,128]{3,1,2,0:T(2,128)S(1)}, u32[]{:S(2)}) copy-start(f32[1,2,4,128]{3,1,2,0:T(2,128)S(1)} %copy.111) | copy-start | bytes 12292
  21.3 60.6 %copy-start.7 = (f32[4,256,64]{2,1,0:T(8,128)}, f32[4,256,64]{2,1,0:T(8,128)S(1)}, u32[]{:S(2)}) copy-start(f32[4,256,64]{2,1,0:T(8,128)S(1)} %get-tuple-element.58) | copy-start | bytes 786436
  21.3 60.6 %copy-start.8 = (f32[4,256,64]{2,1,0:T(8,128)}, f32[4,256,64]{2,1,0:T(8,128)S(1)}, u32[]{:S(2)}) copy-start(f32[4,256,64]{2,1,0:T(8,128)S(1)} %get-tuple-element.59) | copy-start | bytes 786436
  84.6 1.2 copy-start.12
  85.8 2.1 copy-start.20
  87.8 171.1 %reduce-scatter.11.cloned.1.call-start = ((), (), s32[]{:S(2)}) async-start(), calls=%async_computation.13 | async-start | bytes 5242880 | tf_op jit(solution)/shard_map/reduce_scatter | solution.py:88
  97.9 57.8 %copy-start.9 = (bf16[4,256,4,64]{3,1,2,0:T(8,128)(2,1)S(1)}, bf16[4,256,4,64]{3,1,2,0:T(8,128)(2,1)}, u32[]{:S(2)}) copy-start(bf16[4,256,4,64]{3,1,2,0:T(8,128)(2,1)} %get-tuple-element.32) | copy-start | bytes 1572868
  150.5 5.3 copy-start.10
  155.8 8.5 copy-start.4
  182.0 133.5 %all-gather.24.cloned.1.call-start = ((), (), s32[]{:S(2)}) async-start(), calls=%async_computation.17 | async-start | bytes 9437184 | tf_op jit(solution)/shard_map/all_gather | solution.py:81
  184.4 187.2 %all-gather.22.cloned.1.call-start = ((), (), s32[]{:S(2)}) async-start(), calls=%async_computation.16 | async-start | bytes 9437184 | tf_op jit(solution)/shard_map/all_gather | solution.py:75
  186.8 267.7 %all-gather.18.cloned.1.call-start = ((), (), s32[]{:S(2)}) async-start(), calls=%async_computation.14 | async-start | bytes 5242880 | tf_op jit(solution)/shard_map/all_gather | solution.py:94
  263.8 245.8 %all-gather.20.cloned.1.call-start = ((), (), s32[]{:S(2)}) async-start(), calls=%async_computation.15 | async-start | bytes 9437184 | tf_op jit(solution)/shard_map/all_gather | solution.py:75
  266.2 368.3 %reduce-scatter.13.cloned.1.call-start = ((), (), s32[]{:S(2)}) async-start(), calls=%async_computation.18 | async-start | bytes 5242880 | tf_op jit(solution)/shard_map/reduce_scatter | solution.py:88
  509.7 14.7 copy-start.17
  557.6 156.4 %reduce-scatter.15.cloned.1.call-start = ((), (), s32[]{:S(2)}) async-start(), calls=%async_computation.20 | async-start | bytes 5242880 | tf_op jit(solution)/shard_map/reduce_scatter | solution.py:88
  557.6 12.7 copy-start.27
  583.2 130.7 %copy-start.3 = (bf16[256,2048]{1,0:T(8,128)(2,1)S(1)}, bf16[256,2048]{1,0:T(8,128)(2,1)}, u32[]{:S(2)}) copy-start(bf16[256,2048]{1,0:T(8,128)(2,1)} %reduce-scatter.11.cloned.1.call-done) | copy-start | bytes 3145732
  583.3 220.6 %all-gather.28.cloned.1.call-start = ((), (), s32[]{:S(2)}) async-start(), calls=%async_computation.21 | async-start | bytes 5242880 | tf_op jit(solution)/shard_map/all_gather | solution.py:94
  714.0 5.1 copy-start.5
  722.5 197.9 %reduce-scatter.17.cloned.1.call-start = ((), (), s32[]{:S(2)}) async-start(), calls=%async_computation.22 | async-start | bytes 10485760 | tf_op jit(solution)/shard_map/reduce_scatter | solution.py:226
  824.0 12.9 copy-start.2
  850.5 177.0 %reduce-scatter.19.cloned.1.call-start = ((), (), s32[]{:S(2)}) async-start(), calls=%async_computation.23 | async-start | bytes 5242880 | tf_op jit(solution)/shard_map/reduce_scatter | solution.py:88
  935.9 2.6 copy-start.14
  950.6 152.3 %reduce-scatter.25.cloned.1.call-start = ((), (), s32[]{:S(2)}) async-start(), calls=%async_computation.27 | async-start | bytes 9437184 | tf_op jit(solution)/shard_map/reduce_scatter | solution.py:196
  964.9 212.8 %reduce-scatter.27.cloned.1.call-start = ((), (), s32[]{:S(2)}) async-start(), calls=%async_computation.28 | async-start | bytes 9437184 | tf_op jit(solution)/shard_map/reduce_scatter | solution.py:196
  979.1 273.2 %reduce-scatter.29.cloned.1.call-start = ((), (), s32[]{:S(2)}) async-start(), calls=%async_computation.29 | async-start | bytes 9437184 | tf_op jit(solution)/shard_map/reduce_scatter | solution.py:196
  993.5 1.2 copy-start.16
  993.5 341.0 %all-gather.26.cloned.1.call-start = ((), (), s32[]{:S(2)}) async-start(), calls=%async_computation.19 | async-start | bytes 5242880 | tf_op jit(solution)/shard_map/all_gather | solution.py:94
  994.1 6.6 copy-start.21
  994.1 33.4 %copy-start.19 = (f32[1,2048]{1,0:T(1,128)S(1)}, f32[1,2048]{1,0:T(1,128)}, u32[]{:S(2)}) copy-start(f32[1,2048]{1,0:T(1,128)} %copy-done.18) | copy-start | bytes 24580
  994.2 383.7 %reduce-scatter.23.cloned.1.call-start = ((), (), s32[]{:S(2)}) async-start(), calls=%async_computation.26 | async-start | bytes 2359296 | tf_op jit(solution)/shard_map/reduce_scatter | solution.py:196
  1000.6 32.8 %copy-start.24 = (f32[1,2,4,128]{3,1,2,0:T(2,128)S(1)}, f32[1,2,4,128]{3,1,2,0:T(2,128)}, u32[]{:S(2)}) copy-start(f32[1,2,4,128]{3,1,2,0:T(2,128)} %copy-done.23) | copy-start | bytes 12292
  1000.7 510.1 %all-reduce.3.cloned.1.call-start = ((), (), s32[]{:S(2)}) async-start(), calls=%async_computation.30 | async-start | bytes 1056768
  1032.6 0.8 copy-start.15
  1033.4 543.3 %reduce-scatter.21.cloned.1.call-start = ((), (), s32[]{:S(2)}) async-start(), calls=%async_computation.25 | async-start | bytes 7077888 | tf_op jit(solution)/shard_map/reduce_scatter | solution.py:196
  1044.8 1.4 copy-start.6
  1044.8 1.9 copy-start.13
  1044.8 614.8 %all-gather.30.cloned.1.call-start = ((), (), s32[]{:S(2)}) async-start(), calls=%async_computation.24 | async-start | bytes 5242880 | tf_op jit(solution)/shard_map/all_gather | solution.py:94
  1659.7 4.9 copy-start.11
  1659.7 7.0 copy-start.1
Sparse Core Ops, SparseCore 0:
  10.5 48.1 all-gather.11
  61.1 27.7 all-gather.15
  91.0 59.3 all-gather.13
  182.1 76.7 reduce-scatter.10
  260.7 54.7 all-gather.23
  317.2 54.2 all-gather.21
  373.7 80.7 all-gather.17
  456.9 52.7 all-gather.19
  557.7 76.7 reduce-scatter.12
  636.7 77.2 reduce-scatter.14
  722.6 81.2 all-gather.27
  850.6 69.7 reduce-scatter.16
  950.7 76.7 reduce-scatter.18
  1030.8 72.0 reduce-scatter.24
  1106.2 71.4 reduce-scatter.26
  1181.0 71.2 reduce-scatter.28
  1253.7 80.7 all-gather.25
  1338.2 39.6 reduce-scatter.22
  1383.1 127.6 all-reduce.2
  1514.0 62.6 reduce-scatter.20
  1578.9 80.7 all-gather.29
